TPU v7x, 32 devices: a whole 2x2x4 slice. The times are simulated.
32 devices in a mesh: row: 4 (over x, core), col: 8 (over z, y).
Axes of the slice: x: 2, y: 2, z: 4, core: 2. Of those that a mesh axis runs over, the one named last changes fastest.
Arguments:
- pooled: bfloat16 [2048, 1152], P(('row', 'col')), may hold values from -32 to 32
- hidden: bfloat16 [2048, 4304], P(('row', 'col')), may hold values from -6 to 6
- text: bfloat16 [2048, 1152], P(('row', 'col')), may hold values from -12 to 12
- weight: float32 [1152, 4304], P('col', 'row'), may hold values from -0.09375 to 0.09375
- row_moment: float32 [1152], P('col'), may hold values from 1e-07 to 1e-05
- col_moment: float32 [4304], P('row'), may hold values from 1e-07 to 1e-05
- log_scale: float32 [], replicated, may hold values from 4.2 to 4.8
- bias: float32 [], replicated, may hold values from -16 to -12
Outputs:
- update: float32 [1152, 4304], P('col', 'row')
- new_row: float32 [1152], P('col')
- new_col: float32 [4304], P('row')
- loss: float32 [], replicated
All inputs are finite; a program needn't handle non-finite values.
Results may differ from a plain program's by a relative error of at most 0.004.
Values may be sent and summed in bfloat16 or wider, within the bound.
A program may use at most 128 MiB of HBM per device.

v0:
```python
import jax
import jax.numpy as jnp
from jax import lax
from jax.sharding import PartitionSpec as P

D = 1152
FF = 4304
EPSILON = 1e-06
DECAY_RATE = 0.8
CLIP_LEVEL = 1.0
FLOOR_VALUE = 1e-30


def over_row_index(positions, column, tokens, columns):
    return (positions // tokens * columns + column) * tokens + positions % tokens


def over_col_index(positions, row_place, tokens, columns):
    return row_place * columns * tokens + positions


def pair_tile(images, image_ids, texts, text_ids, logit_scale, bias, batch_total):
    logits = logit_scale * jnp.dot(images, texts.T, preferred_element_type=jnp.float32) + bias
    label_sign = jnp.where(
        image_ids[:, None] == text_ids[None, :], jnp.float32(1.0), jnp.float32(-1.0)
    )
    loss_sum = jnp.sum(jax.nn.softplus(-label_sign * logits))
    grad_logits = (-label_sign * jax.nn.sigmoid(-label_sign * logits) / batch_total).astype(
        jnp.bfloat16
    )
    return (loss_sum, logit_scale * jnp.dot(grad_logits, texts, preferred_element_type=jnp.float32))


def per_device(pooled, hidden, text, weight, row_moment, col_moment, log_scale, bias):
    rows_count = lax.axis_size("row")
    cols_count = lax.axis_size("col")
    row_place = lax.axis_index("row")
    col_place = lax.axis_index("col")
    tokens = pooled.shape[0]
    batch_total = tokens * rows_count * cols_count
    split_hidden = lax.all_to_all(hidden, "row", split_axis=1, concat_axis=0, tiled=True)
    hidden_cols = split_hidden.shape[1]
    weight_half = weight.astype(jnp.bfloat16)
    grouped = split_hidden.reshape(rows_count, tokens, hidden_cols)
    hidden_all = lax.all_gather(grouped, "col", axis=1, tiled=True).reshape(
        batch_total, hidden_cols
    )
    partial_proj = lax.dot_general(
        weight_half, hidden_all, (((1,), (1,)), ((), ())), preferred_element_type=jnp.float32
    )
    summed = lax.psum_scatter(partial_proj, "row", scatter_dimension=1, tiled=True)
    projected = lax.all_to_all(summed, "col", split_axis=1, concat_axis=0, tiled=True).T
    mixed_rows = pooled.astype(jnp.float32) + projected
    length = jnp.sqrt(jnp.sum(mixed_rows * mixed_rows, axis=1, keepdims=True) + EPSILON)
    image_unit = mixed_rows / length
    images = image_unit.astype(jnp.bfloat16)
    text_float = text.astype(jnp.float32)
    text_units = (
        text_float / jnp.sqrt(jnp.sum(text_float * text_float, axis=1, keepdims=True) + EPSILON)
    ).astype(jnp.bfloat16)
    logit_scale = jnp.exp(log_scale)
    image_rows = lax.all_gather(images, "row", axis=0, tiled=True)
    image_ids = over_row_index(
        jnp.arange(image_rows.shape[0], dtype=jnp.int32), col_place, tokens, cols_count
    )
    piece = lax.all_gather(text_units, "col", axis=0, tiled=True)
    text_ids = over_col_index(
        jnp.arange(piece.shape[0], dtype=jnp.int32), row_place, tokens, cols_count
    )
    loss_local, unit_part = pair_tile(
        image_rows, image_ids, piece, text_ids, logit_scale, bias, batch_total
    )
    unit_grad = lax.psum_scatter(unit_part, "row", scatter_dimension=0, tiled=True)
    mixed_grad = (
        (unit_grad - image_unit * jnp.sum(image_unit * unit_grad, axis=1, keepdims=True)) / length
    ).astype(jnp.bfloat16)
    grad_cols = lax.all_to_all(mixed_grad.T, "col", split_axis=0, concat_axis=1, tiled=True)
    gradient = jnp.dot(
        lax.all_gather(grad_cols, "row", axis=1, tiled=True),
        hidden_all,
        preferred_element_type=jnp.float32,
    )
    squared = gradient * gradient + FLOOR_VALUE
    row_sum = lax.psum(jnp.sum(squared, axis=1), "row")
    col_sum = lax.psum(jnp.sum(squared, axis=0), "col")
    new_row = DECAY_RATE * row_moment + (1.0 - DECAY_RATE) * row_sum / FF
    new_col = DECAY_RATE * col_moment + (1.0 - DECAY_RATE) * col_sum / D
    second = new_row[:, None] * new_col[None, :]
    raw_update = gradient / jnp.sqrt(second)
    loss_total = lax.psum(loss_local, ("row", "col"))
    update_total = lax.psum(jnp.sum(raw_update * raw_update), ("row", "col"))
    update_rms = jnp.sqrt(update_total / (D * FF))
    update = raw_update / jnp.maximum(1.0, update_rms / CLIP_LEVEL)
    loss = loss_total / batch_total
    return (update, new_row, new_col, loss)


def solution(mesh):
    return jax.shard_map(
        per_device,
        mesh=mesh,
        in_specs=(
            P(("row", "col"), None),
            P(("row", "col"), None),
            P(("row", "col"), None),
            P("col", "row"),
            P("col"),
            P("row"),
            P(),
            P(),
        ),
        out_specs=(P("col", "row"), P("col"), P("row"), P()),
        check_vma=False,
    )
```

profile of v0, /device:TPU:12, one launch (start us, length us, event | category | flops | bytes accessed | tf_op | source)
XLA Modules:
  0.0 324.7 jit_solution(10579943734243616240)
XLA Ops:
  7.2 1.5 all_to_all.40
  8.8 12.1 %all_to_all.54 = bf16[64,4,1076]{2,0,1:T(8,128)(2,1)S(1)} all-to-all(bf16[64,4,1076]{2,0,1:T(8,128)(2,1)S(1)} %copy.22), channel_id=1, replica_groups=mesh['row'=4,'col'=8] {'row'}, dimensions={1} | all-to-all | bytes 1101824 | tf_op jit(solution)/shard_map/all_to_all | solution.py:41
  20.9 1.3 copy.23
  22.2 78.1 %all-gather.3.cloned.1.call-done = bf16[4,512,1076]{2,0,1:T(4,128)(2,1)} async-done(((bf16[4,64,1076]{2,0,1:T(4,128)(2,1)}), bf16[4,512,1076]{2,0,1:T(4,128)(2,1)}) %all-gather.3.cloned.1.call-update) | async-done | bytes 4407312 | tf_op jit(solution)/shard_map/all_gather | solution.py:45
  100.3 10.4 %copy.24 = bf16[4,512,1076]{1,0,2:T(4,128)(2,1)} copy(bf16[4,512,1076]{2,0,1:T(4,128)(2,1)} %all-gather.3.cloned.1.call-done) | data formatting | bytes 8814592 | tf_op jit(solution)/shard_map/all_gather | solution.py:45
  110.7 3.9 %pad = bf16[1080,4,512]{2,1,0:T(4,128)(2,1)S(1)} pad(bf16[1076,4,512]{2,1,0:T(4,128)(2,1)} %bitcast.38, bf16[]{:T(256)} %constant.79), padding=0_4x0_0x0_0 | pad | bytes 8830978
  114.6 1.9 copy.31
  116.5 2.0 copy-done
  118.5 2.2 fusion.6
  122.6 23.8 %reduce-scatter.3.cloned.1.call-done = f32[144,512]{1,0:T(8,128)} async-done(((f32[144,2048]{1,0:T(8,128)}), f32[144,512]{1,0:T(8,128)}) %reduce-scatter.3.cloned.1.call-update) | async-done | bytes 294928 | tf_op jit(solution)/shard_map/reduce_scatter | solution.py:51
  146.4 2.0 copy.29
  148.3 6.1 %all-to-all-start.1 = ((f32[144,8,64]{0,2,1:T(8,128)}), f32[144,8,64]{0,2,1:T(8,128)S(1)}, u32[]{:S(2)}, u32[]{:S(2)}) async-start(f32[144,8,64]{0,2,1:T(8,128)} %bitcast.1), calls=%async_computation.2 | async-start | bytes 1048576 | tf_op jit(solution)/shard_map/all_to_all | solution.py:52
  155.8 14.4 %all-to-all-done.1 = f32[144,8,64]{0,2,1:T(8,128)S(1)} async-done(((f32[144,8,64]{0,2,1:T(8,128)}), f32[144,8,64]{0,2,1:T(8,128)S(1)}, u32[]{:S(2)}, u32[]{:S(2)}) %all-to-all-start.1) | async-done | bytes 294944 | tf_op jit(solution)/shard_map/all_to_all | solution.py:52
  171.0 7.1 %all_gather.13 = bf16[256,1152]{1,0:T(8,128)(2,1)S(1)} all-gather(bf16[64,1152]{1,0:T(8,128)(2,1)S(1)} %fusion.26), channel_id=1, replica_groups=mesh['row'=4,'col'=8] {'row'}, dimensions={0}, use_global_device_ids=true | all-gather | bytes 737280 | tf_op jit(solution)/shard_map/all_gather | solution.py:62
  178.1 12.6 %all-gather.5.cloned.1.call-done = bf16[512,1152]{1,0:T(8,128)(2,1)} async-done(((bf16[64,1152]{1,0:T(8,128)(2,1)}), bf16[512,1152]{1,0:T(8,128)(2,1)}) %all-gather.5.cloned.1.call-update) | async-done | bytes 1179664 | tf_op jit(solution)/shard_map/all_gather | solution.py:66
  190.6 2.9 fusion.5
  193.5 1.6 convolution_multiply_fusion
  195.1 26.1 %reduce-scatter.5.cloned.1.call-done = f32[64,1152]{1,0:T(8,128)} async-done(((f32[256,1152]{1,0:T(8,128)}), f32[64,1152]{1,0:T(8,128)}) %reduce-scatter.5.cloned.1.call-update) | async-done | bytes 294928 | tf_op jit(solution)/shard_map/reduce_scatter | solution.py:73
  223.9 12.6 %all_to_all.55 = bf16[8,144,64]{1,2,0:T(8,128)(2,1)S(1)} all-to-all(bf16[8,144,64]{1,2,0:T(8,128)(2,1)S(1)} %copy.27), channel_id=1, replica_groups=mesh['row'=4,'col'=8] {'col'}, dimensions={0} | all-to-all | bytes 294912 | tf_op jit(solution)/shard_map/all_to_all | solution.py:77
  236.6 6.7 %all_gather.15 = bf16[144,2048]{1,0:T(8,128)(2,1)S(1)} all-gather(bf16[144,512]{1,0:T(8,128)(2,1)S(1)} %copy.30), channel_id=1, replica_groups=mesh['row'=4,'col'=8] {'row'}, dimensions={1}, use_global_device_ids=true | all-gather | bytes 737280 | tf_op jit(solution)/shard_map/all_gather | solution.py:79
  243.3 4.1 %fusion.3 = (f32[144]{0:T(256)S(1)}, f32[1076]{0:T(1024)S(1)}, f32[144,1076]{1,0:T(8,128)S(1)}) fusion(bf16[144,2048]{1,0:T(8,128)(2,1)S(1)} %all_gather.15, bf16[2048,1076]{0,1:T(8,128)(2,1)} %bitcast.36), kind=kOutput, calls=%fused_computation.9 | convolution fusion | flops 635269184 | bytes 5621776 | tf_op jit(solution)/shard_map/dot_general | solution.py:78
  247.3 16.7 %psum.29 = f32[1076]{0:T(1024)S(1)} all-reduce(f32[1076]{0:T(1024)S(1)} %get-tuple-element.5), channel_id=1, replica_groups=mesh['row'=4,'col'=8] {'col'}, use_global_device_ids=true, to_apply=%region_8.9 | all-reduce | flops 1076 | bytes 8608 | tf_op jit(solution)/shard_map/psum | solution.py:85
  264.0 5.7 %psum.28 = f32[144]{0:T(256)S(1)} all-reduce(f32[144]{0:T(256)S(1)} %get-tuple-element.4), channel_id=1, replica_groups=mesh['row'=4,'col'=8] {'row'}, use_global_device_ids=true, to_apply=%region_6.7 | all-reduce | flops 144 | bytes 1152 | tf_op jit(solution)/shard_map/psum | solution.py:84
  270.7 44.0 %all-reduce = (f32[]{:T(128)}, f32[]{:T(128)}) all-reduce(f32[]{:T(128)} %multiply_reduce_fusion, f32[]{:T(128)} %get-tuple-element.9), channel_id=1, replica_groups=mesh['row'=4,'col'=8] {'row','col'}, use_global_device_ids=true, to_apply=%region_10.11 | all-reduce | flops 2 | bytes 16 | tf_op jit(solution)/shard_map/psum | solution.py:91
  (45 shorter events, 7.5 us)
Async XLA Ops:
  7.2 93.2 %all-gather.3.cloned.1.call-start = ((), (), s32[]{:S(2)}) async-start(), calls=%async_computation.5 | async-start | bytes 5308416 | tf_op jit(solution)/shard_map/all_gather | solution.py:45
  22.2 124.2 %reduce-scatter.3.cloned.1.call-start = ((), (), s32[]{:S(2)}) async-start(), calls=%async_computation.6 | async-start | bytes 1474560 | tf_op jit(solution)/shard_map/reduce_scatter | solution.py:51
  114.6 3.9 %copy-start.2 = (f32[144,1076]{1,0:T(8,128)S(1)}, f32[144,1076]{1,0:T(8,128)}, u32[]{:S(2)}) copy-start(f32[144,1076]{1,0:T(8,128)} %param.11) | copy-start | bytes 1859332
  116.5 2.0 copy-start
  120.8 0.9 copy-start.3
  120.8 69.8 %all-gather.5.cloned.1.call-start = ((), (), s32[]{:S(2)}) async-start(), calls=%async_computation.7 | async-start | bytes 1327104 | tf_op jit(solution)/shard_map/all_gather | solution.py:66
  148.3 21.8 %all-to-all-start.1 = ((f32[144,8,64]{0,2,1:T(8,128)}), f32[144,8,64]{0,2,1:T(8,128)S(1)}, u32[]{:S(2)}, u32[]{:S(2)}) async-start(f32[144,8,64]{0,2,1:T(8,128)} %bitcast.1), calls=%async_computation.2 | async-start | bytes 1048576 | tf_op jit(solution)/shard_map/all_to_all | solution.py:52
  154.4 16.3 %copy-start.1 = (bf16[64,1152]{1,0:T(8,128)(2,1)S(1)}, bf16[64,1152]{1,0:T(8,128)(2,1)}, u32[]{:S(2)}) copy-start(bf16[64,1152]{1,0:T(8,128)(2,1)} %param.8) | copy-start | bytes 442372
  154.4 66.8 %reduce-scatter.5.cloned.1.call-start = ((), (), s32[]{:S(2)}) async-start(), calls=%async_computation.8 | async-start | bytes 1474560 | tf_op jit(solution)/shard_map/reduce_scatter | solution.py:73
  190.6 2.9 copy-start.8
  243.3 26.4 %copy-start.6 = (f32[1076]{0:T(1024)S(1)}, f32[1076]{0:T(1024)}, u32[]{:S(2)}) copy-start(f32[1076]{0:T(1024)} %param.13) | copy-start | bytes 12916
  243.3 26.4 %copy-start.7 = (f32[144]{0:T(256)S(1)}, f32[144]{0:T(256)}, u32[]{:S(2)}) copy-start(f32[144]{0:T(256)} %param.12) | copy-start | bytes 1732
  269.7 47.3 %copy-start.4 = (f32[1076]{0:T(1024)}, f32[1076]{0:T(1024)S(1)}, u32[]{:S(2)}) copy-start(f32[1076]{0:T(1024)S(1)} %multiply_add_fusion.1) | copy-start | bytes 12916
  269.7 47.3 %copy-start.5 = (f32[144]{0:T(256)}, f32[144]{0:T(256)S(1)}, u32[]{:S(2)}) copy-start(f32[144]{0:T(256)S(1)} %multiply_add_fusion.2) | copy-start | bytes 1732
Sparse Core Ops, SparseCore 0:
  22.3 78.0 all-gather.2
  120.9 25.4 reduce-scatter.2
  148.6 41.9 all-gather.4
  195.3 25.9 reduce-scatter.4
where the time goes:
time: 326 us; the launch traced here: 325 us
  waiting for transfers between devices  155 us (48%)
  blocking collectives  105 us (32%)
  local copies, waits for them, and re-layouts  24.9 us (8%)
  between operations  17.8 us (5%)
  matrix products  10.8 us (3%)
  starting transfers between devices  6.18 us (2%)
  other arithmetic  5.36 us (2%)
    all_gather x1, waiting for transfers between devices, per_device(): lax.all_gather(grouped, 'col', axis=1, tiled=True)  78.1 us
    psum x1, blocking collectives, per_device(): update_total = lax.psum(jnp.sum(raw_update * raw_update), ('row', 'col'))  44 us
    reduce_scatter x1, waiting for transfers between devices, per_device(): lax.psum_scatter(unit_part, 'row', scatter_dimension=0, tiled=True)  26.1 us
    reduce_scatter x1, waiting for transfers between devices, per_device(): lax.psum_scatter(partial_proj, 'row', scatter_dimension=1, tiled=True)  23.8 us
    psum x1, blocking collectives, per_device(): col_sum = lax.psum(jnp.sum(squared, axis=0), 'col')  16.7 us
    all_to_all x1, waiting for transfers between devices, per_device(): lax.all_to_all(summed, 'col', split_axis=1, concat_axis=0, tiled=True)  14.4 us
    all_to_all x1, blocking collectives, per_device(): lax.all_to_all(mixed_grad.T, 'col', split_axis=0, concat_axis=1, tiled=True)  12.6 us
    all_gather x1, waiting for transfers between devices, per_device(): piece = lax.all_gather(text_units, 'col', axis=0, tiled=True)  12.6 us
  transfers between devices with their start and end apart: 5, of which 5 were waited for; matrix products, arithmetic and copies ran while one was open for 1% of the time, Pallas kernels for 0%

commit v1 on v0

--- a/solution.py
+++ b/solution.py
@@ -82,7 +82,7 @@
     )
     squared = gradient * gradient + FLOOR_VALUE
     row_sum = lax.psum(jnp.sum(squared, axis=1), "row")
-    col_sum = lax.psum(jnp.sum(squared, axis=0), "col")
+    col_sum = jnp.sum(lax.all_gather(jnp.sum(squared, axis=0), "col"), axis=0)
     new_row = DECAY_RATE * row_moment + (1.0 - DECAY_RATE) * row_sum / FF
     new_col = DECAY_RATE * col_moment + (1.0 - DECAY_RATE) * col_sum / D
     second = new_row[:, None] * new_col[None, :]

time: 326 us -> 343 us (1.052)
  starting transfers between devices: 6.18 us -> 12.2 us
  waiting for transfers between devices: 155 us -> 160 us
    unnamed x0 -> x1, blocking collectives: none -> 30.8 us
    psum x1 -> x0, blocking collectives: 16.7 us -> none  [per_device(): col_sum = lax.psum(jnp.sum(squared, axis=0), 'col')]
    all_to_all x1 -> x0, blocking collectives: 12.6 us -> none  [per_device(): lax.all_to_all(mixed_grad.T, 'col', split_axis=0, concat_axis=1, tiled=True)]
    all_to_all x0 -> x1, starting transfers between devices: none -> 6.02 us  [per_device(): lax.all_to_all(mixed_grad.T, 'col', split_axis=0, concat_axis=1, tiled=True)]
    all_to_all x0 -> x1, waiting for transfers between devices: none -> 5.53 us  [per_device(): lax.all_to_all(mixed_grad.T, 'col', split_axis=0, concat_axis=1, tiled=True)]
    unnamed x20 -> x25, local copies, waits for them, and re-layouts: 8.66 us -> 9.58 us
  transfers between devices with their start and end apart: 5 -> 6, of which waited for: 5 -> 6; matrix products, arithmetic and copies ran while one was open for 1% -> 1% of each run, Pallas kernels for 0% -> 0%
where the time goes in v1:
time: 343 us; the launch traced here: 342 us
  waiting for transfers between devices  160 us (47%)
  blocking collectives  108 us (31%)
  local copies, waits for them, and re-layouts  26.6 us (8%)
  between operations  18.4 us (5%)
  starting transfers between devices  12.2 us (4%)
  matrix products  10.8 us (3%)
  other arithmetic  5.38 us (2%)
    all_gather x1, waiting for transfers between devices, per_device(): lax.all_gather(grouped, 'col', axis=1, tiled=True)  78.1 us
    psum x1, blocking collectives, per_device(): update_total = lax.psum(jnp.sum(raw_update * raw_update), ('row', 'col'))  45.6 us
    unnamed x1, blocking collectives  30.8 us
    reduce_scatter x1, waiting for transfers between devices, per_device(): lax.psum_scatter(unit_part, 'row', scatter_dimension=0, tiled=True)  26.1 us
    reduce_scatter x1, waiting for transfers between devices, per_device(): lax.psum_scatter(partial_proj, 'row', scatter_dimension=1, tiled=True)  23.8 us
    all_to_all x1, waiting for transfers between devices, per_device(): lax.all_to_all(summed, 'col', split_axis=1, concat_axis=0, tiled=True)  14.4 us
    all_gather x1, waiting for transfers between devices, per_device(): piece = lax.all_gather(text_units, 'col', axis=0, tiled=True)  12.6 us
    all_to_all x1, blocking collectives, per_device(): lax.all_to_all(hidden, 'row', split_axis=1, concat_axis=0, tiled=True)  12.1 us
  transfers between devices with their start and end apart: 6, of which 6 were waited for; matrix products, arithmetic and copies ran while one was open for 1% of the time, Pallas kernels for 0%

profile of v1, /device:TPU:12, one launch (start us, length us, event | category | flops | bytes accessed | tf_op | source)
XLA Modules:
  0.0 341.8 jit_solution(15224812953323428541)
XLA Ops:
  7.2 1.5 all_to_all.40
  8.8 12.1 %all_to_all.54 = bf16[64,4,1076]{2,0,1:T(8,128)(2,1)S(1)} all-to-all(bf16[64,4,1076]{2,0,1:T(8,128)(2,1)S(1)} %copy.29), channel_id=1, replica_groups=mesh['row'=4,'col'=8] {'row'}, dimensions={1} | all-to-all | bytes 1101824 | tf_op jit(solution)/shard_map/all_to_all | solution.py:41
  22.2 78.1 %all-gather.4.cloned.1.call-done = bf16[4,512,1076]{2,0,1:T(4,128)(2,1)} async-done(((bf16[4,64,1076]{2,0,1:T(4,128)(2,1)}), bf16[4,512,1076]{2,0,1:T(4,128)(2,1)}) %all-gather.4.cloned.1.call-update) | async-done | bytes 4407312 | tf_op jit(solution)/shard_map/all_gather | solution.py:45
  100.3 10.4 %copy.31 = bf16[4,512,1076]{1,0,2:T(4,128)(2,1)} copy(bf16[4,512,1076]{2,0,1:T(4,128)(2,1)} %all-gather.4.cloned.1.call-done) | data formatting | bytes 8814592 | tf_op jit(solution)/shard_map/all_gather | solution.py:45
  110.7 3.9 %pad = bf16[1080,4,512]{2,1,0:T(4,128)(2,1)S(1)} pad(bf16[1076,4,512]{2,1,0:T(4,128)(2,1)} %bitcast.39, bf16[]{:T(256)} %constant.85), padding=0_4x0_0x0_0 | pad | bytes 8830978
  114.6 1.9 copy.38
  116.5 2.0 copy-done
  118.5 2.2 fusion.6
  122.6 23.8 %reduce-scatter.3.cloned.1.call-done = f32[144,512]{1,0:T(8,128)} async-done(((f32[144,2048]{1,0:T(8,128)}), f32[144,512]{1,0:T(8,128)}) %reduce-scatter.3.cloned.1.call-update) | async-done | bytes 294928 | tf_op jit(solution)/shard_map/reduce_scatter | solution.py:51
  146.4 2.0 copy.36
  148.3 6.1 %all-to-all-start.1 = ((f32[144,8,64]{0,2,1:T(8,128)}), f32[144,8,64]{0,2,1:T(8,128)S(1)}, u32[]{:S(2)}, u32[]{:S(2)}) async-start(f32[144,8,64]{0,2,1:T(8,128)} %bitcast.1), calls=%async_computation.2 | async-start | bytes 1048576 | tf_op jit(solution)/shard_map/all_to_all | solution.py:52
  155.8 14.4 %all-to-all-done.1 = f32[144,8,64]{0,2,1:T(8,128)S(1)} async-done(((f32[144,8,64]{0,2,1:T(8,128)}), f32[144,8,64]{0,2,1:T(8,128)S(1)}, u32[]{:S(2)}, u32[]{:S(2)}) %all-to-all-start.1) | async-done | bytes 294944 | tf_op jit(solution)/shard_map/all_to_all | solution.py:52
  171.0 7.1 %all_gather.19 = bf16[256,1152]{1,0:T(8,128)(2,1)S(1)} all-gather(bf16[64,1152]{1,0:T(8,128)(2,1)S(1)} %fusion.26), channel_id=1, replica_groups=mesh['row'=4,'col'=8] {'row'}, dimensions={0}, use_global_device_ids=true | all-gather | bytes 737280 | tf_op jit(solution)/shard_map/all_gather | solution.py:62
  178.1 12.6 %all-gather.6.cloned.1.call-done = bf16[512,1152]{1,0:T(8,128)(2,1)} async-done(((bf16[64,1152]{1,0:T(8,128)(2,1)}), bf16[512,1152]{1,0:T(8,128)(2,1)}) %all-gather.6.cloned.1.call-update) | async-done | bytes 1179664 | tf_op jit(solution)/shard_map/all_gather | solution.py:66
  190.6 2.9 fusion.5
  193.5 1.6 convolution_multiply_fusion
  195.1 26.1 %reduce-scatter.5.cloned.1.call-done = f32[64,1152]{1,0:T(8,128)} async-done(((f32[256,1152]{1,0:T(8,128)}), f32[64,1152]{1,0:T(8,128)}) %reduce-scatter.5.cloned.1.call-update) | async-done | bytes 294928 | tf_op jit(solution)/shard_map/reduce_scatter | solution.py:73
  224.6 6.0 %all-to-all-start.2 = ((bf16[8,144,64]{1,2,0:T(8,128)(2,1)}), bf16[8,144,64]{1,2,0:T(8,128)(2,1)S(1)}, u32[]{:S(2)}, u32[]{:S(2)}) async-start(bf16[8,144,64]{1,2,0:T(8,128)(2,1)} %copy.34), calls=%async_computation.4 | async-start | bytes 524288 | tf_op jit(solution)/shard_map/all_to_all | solution.py:77
  231.9 5.5 %all-to-all-done.2 = bf16[8,144,64]{1,2,0:T(8,128)(2,1)S(1)} async-done(((bf16[8,144,64]{1,2,0:T(8,128)(2,1)}), bf16[8,144,64]{1,2,0:T(8,128)(2,1)S(1)}, u32[]{:S(2)}, u32[]{:S(2)}) %all-to-all-start.2) | async-done | bytes 147488 | tf_op jit(solution)/shard_map/all_to_all | solution.py:77
  237.5 6.7 %all_gather.21 = bf16[144,2048]{1,0:T(8,128)(2,1)S(1)} all-gather(bf16[144,512]{1,0:T(8,128)(2,1)S(1)} %copy.37), channel_id=1, replica_groups=mesh['row'=4,'col'=8] {'row'}, dimensions={1}, use_global_device_ids=true | all-gather | bytes 737280 | tf_op jit(solution)/shard_map/all_gather | solution.py:79
  244.2 4.1 %fusion.3 = (f32[144]{0:T(256)S(1)}, f32[1076]{0:T(1024)S(1)}, f32[144,1076]{1,0:T(8,128)S(1)}) fusion(bf16[144,2048]{1,0:T(8,128)(2,1)S(1)} %all_gather.21, bf16[2048,1076]{0,1:T(8,128)(2,1)} %bitcast.37), kind=kOutput, calls=%fused_computation.9 | convolution fusion | flops 635269184 | bytes 5621776 | tf_op jit(solution)/shard_map/dot_general | solution.py:78
  248.6 30.8 %all-reduce = f32[8608]{0:T(1024)S(1)} all-reduce(f32[8608]{0:T(1024)S(1)} %dynamic-update-slice), channel_id=2, replica_groups=mesh['row'=4,'col'=8] {'col'}, use_global_device_ids=true, to_apply=%add | all-reduce | flops 8608 | bytes 68864
  279.5 5.7 %psum.21 = f32[144]{0:T(256)S(1)} all-reduce(f32[144]{0:T(256)S(1)} %get-tuple-element.4), channel_id=1, replica_groups=mesh['row'=4,'col'=8] {'row'}, use_global_device_ids=true, to_apply=%region_6.7 | all-reduce | flops 144 | bytes 1152 | tf_op jit(solution)/shard_map/psum | solution.py:84
  286.1 45.6 %all-reduce.1 = (f32[]{:T(128)}, f32[]{:T(128)}) all-reduce(f32[]{:T(128)} %multiply_reduce_fusion, f32[]{:T(128)} %get-tuple-element.9), channel_id=1, replica_groups=mesh['row'=4,'col'=8] {'row','col'}, use_global_device_ids=true, to_apply=%region_10.11 | all-reduce | flops 2 | bytes 16 | tf_op jit(solution)/shard_map/psum | solution.py:91
  (53 shorter events, 10.5 us)
Async XLA Ops:
  7.2 93.2 %all-gather.4.cloned.1.call-start = ((), (), s32[]{:S(2)}) async-start(), calls=%async_computation.5 | async-start | bytes 5308416 | tf_op jit(solution)/shard_map/all_gather | solution.py:45
  22.2 124.2 %reduce-scatter.3.cloned.1.call-start = ((), (), s32[]{:S(2)}) async-start(), calls=%async_computation.6 | async-start | bytes 1474560 | tf_op jit(solution)/shard_map/reduce_scatter | solution.py:51
  114.6 3.9 %copy-start.2 = (f32[144,1076]{1,0:T(8,128)S(1)}, f32[144,1076]{1,0:T(8,128)}, u32[]{:S(2)}) copy-start(f32[144,1076]{1,0:T(8,128)} %param.11) | copy-start | bytes 1859332
  116.5 2.0 copy-start
  120.8 0.9 copy-start.3
  120.8 69.8 %all-gather.6.cloned.1.call-start = ((), (), s32[]{:S(2)}) async-start(), calls=%async_computation.7 | async-start | bytes 1327104 | tf_op jit(solution)/shard_map/all_gather | solution.py:66
  148.3 21.8 %all-to-all-start.1 = ((f32[144,8,64]{0,2,1:T(8,128)}), f32[144,8,64]{0,2,1:T(8,128)S(1)}, u32[]{:S(2)}, u32[]{:S(2)}) async-start(f32[144,8,64]{0,2,1:T(8,128)} %bitcast.1), calls=%async_computation.2 | async-start | bytes 1048576 | tf_op jit(solution)/shard_map/all_to_all | solution.py:52
  154.4 16.3 %copy-start.1 = (bf16[64,1152]{1,0:T(8,128)(2,1)S(1)}, bf16[64,1152]{1,0:T(8,128)(2,1)}, u32[]{:S(2)}) copy-start(bf16[64,1152]{1,0:T(8,128)(2,1)} %param.8) | copy-start | bytes 442372
  154.4 66.8 %reduce-scatter.5.cloned.1.call-start = ((), (), s32[]{:S(2)}) async-start(), calls=%async_computation.8 | async-start | bytes 1474560 | tf_op jit(solution)/shard_map/reduce_scatter | solution.py:73
  190.6 2.9 copy-start.8
  222.4 8.2 %copy-start.9 = (u32[32]{0:T(128)S(1)}, u32[32]{0:T(128)}, u32[]{:S(2)}) copy-start(u32[32]{0:T(128)} %constant.81) | copy-start | bytes 388
  224.6 12.8 %all-to-all-start.2 = ((bf16[8,144,64]{1,2,0:T(8,128)(2,1)}), bf16[8,144,64]{1,2,0:T(8,128)(2,1)S(1)}, u32[]{:S(2)}, u32[]{:S(2)}) async-start(bf16[8,144,64]{1,2,0:T(8,128)(2,1)} %copy.34), calls=%async_computation.4 | async-start | bytes 524288 | tf_op jit(solution)/shard_map/all_to_all | solution.py:77
  244.2 41.0 %copy-start.6 = (f32[1076]{0:T(1024)S(1)}, f32[1076]{0:T(1024)}, u32[]{:S(2)}) copy-start(f32[1076]{0:T(1024)} %param.13) | copy-start | bytes 12916
  244.2 41.0 %copy-start.7 = (f32[144]{0:T(256)S(1)}, f32[144]{0:T(256)}, u32[]{:S(2)}) copy-start(f32[144]{0:T(256)} %param.12) | copy-start | bytes 1732
  285.2 48.9 %copy-start.4 = (f32[1076]{0:T(1024)}, f32[1076]{0:T(1024)S(1)}, u32[]{:S(2)}) copy-start(f32[1076]{0:T(1024)S(1)} %multiply_add_fusion.1) | copy-start | bytes 12916
  285.2 48.9 %copy-start.5 = (f32[144]{0:T(256)}, f32[144]{0:T(256)S(1)}, u32[]{:S(2)}) copy-start(f32[144]{0:T(256)S(1)} %multiply_add_fusion.2) | copy-start | bytes 1732
Sparse Core Ops, SparseCore 0:
  22.3 78.0 all-gather.3
  120.9 25.4 reduce-scatter.2
  148.6 41.9 all-gather.5
  195.3 25.9 reduce-scatter.4
